TPU v7x, 128 devices: a whole 4x4x4 slice. The times are simulated.
128 devices in a mesh: dp: 2 (over x_lo), expert: 32 (over y, z, core), tensor: 2 (over x_hi).
Axes of the slice: x: 4 (x_hi: 2, x_lo: 2; x = x_hi * 2 + x_lo), y: 4, z: 4, core: 2. Of those that a mesh axis runs over, the one named last changes fastest.
Arguments:
- tokens: bfloat16 [8192, 2048], P(('dp', 'expert')), may hold values from -6 to 6
- norm_gain: float32 [2048], replicated, may hold values from 0.1 to 1.9
- router: bfloat16 [2048, 32], replicated, may hold values from -0.125 to 0.125
- expert_ids: int32 [8192, 4], P(('dp', 'expert')), may hold values from 0 to 31, all different within a row; in each aligned block of 128 rows (0 to 127, 128 to 255, ...) at most 20 rows name the same one
- modality: int32 [8192], P(('dp', 'expert')), may hold values from 0 to 1, as said below
- expert_gate: bfloat16 [32, 2048, 1408], P('expert', None, 'tensor'), may hold values from -0.125 to 0.125
- expert_up: bfloat16 [32, 2048, 1408], P('expert', None, 'tensor'), may hold values from -0.125 to 0.125
- expert_down: bfloat16 [32, 1408, 2048], P('expert', 'tensor'), may hold values from -0.15625 to 0.15625
- shared_gate: bfloat16 [2, 2048, 704], P(None, None, ('dp', 'tensor')), may hold values from -0.125 to 0.125
- shared_up: bfloat16 [2, 2048, 704], P(None, None, ('dp', 'tensor')), may hold values from -0.125 to 0.125
- shared_down: bfloat16 [2, 704, 2048], P(None, ('dp', 'tensor')), may hold values from -0.21875 to 0.21875
Outputs:
- mixed: bfloat16 [8192, 2048], P(('dp', 'expert'), 'tensor')
Inputs may be any that keep to these rules, and one draw needn't show every extreme that they name: `expert_ids`: each token names 4 different experts; among the 128 tokens of one device (aligned blocks of rows) no expert is named by more than 20 tokens, and some expert reaches 20. `modality`: within each aligned block of 128 tokens the image patches form one run (taken cyclically) that covers from an eighth to seven eighths of the block.
All inputs are finite; a program needn't handle non-finite values.
Results may differ from a plain program's by a relative error of at most 0.0073.
Values may be sent and summed in bfloat16 or wider, within the bound.
A program may use at most 128 MiB of HBM per device.

v0:
```python
import jax
import jax.numpy as jnp
from jax import lax
from jax.sharding import PartitionSpec as P

epsilon = 1e-06


def in_blocks(x, dim, size):
    lengths = x.shape
    tiles = x.reshape(*lengths[:dim], size, lengths[dim] // size, *lengths[dim + 1 :])
    return jnp.moveaxis(tiles, dim, 0)


def sent_and_summed(x, axis, dim):
    tiles = in_blocks(x, dim, lax.axis_size(axis))
    arrived = lax.all_to_all(tiles, axis, split_axis=0, concat_axis=0, tiled=True)
    return arrived.astype(jnp.float32).sum(axis=0)


def sent_to_all(x, axis):
    size = lax.axis_size(axis)
    return lax.all_to_all(jnp.broadcast_to(x[None], (size, *x.shape)), axis, 0, 0, tiled=True)


def joined_along(tiles, dim):
    lengths = list(tiles.shape[1:])
    lengths[dim] *= tiles.shape[0]
    return jnp.moveaxis(tiles, 0, dim).reshape(lengths)


def collect(x, axis, dim):
    tiles = sent_to_all(x, axis)
    return joined_along(tiles, dim)


def rms_normed(tokens, norm_gain):
    values = tokens.astype(jnp.float32)
    inv_scale = lax.rsqrt(jnp.mean(values * values, axis=-1, keepdims=True) + epsilon)
    return (values * inv_scale * norm_gain).astype(jnp.bfloat16)


def route_weights(normed, router, expert_ids):
    logits = jnp.dot(normed, router, preferred_element_type=jnp.float32)
    chosen = jnp.take_along_axis(logits, expert_ids, axis=1)
    scores = jax.nn.sigmoid(chosen)
    return scores / jnp.sum(scores, axis=1, keepdims=True)


def capacity_slots(expert_ids, expert_count, block_rows):
    row_count, top_count = expert_ids.shape
    onehot = (
        expert_ids[:, :, None] == jnp.arange(expert_count, dtype=jnp.int32)[None, None, :]
    ).astype(jnp.int32)
    grouped = onehot.reshape(row_count // block_rows, block_rows * top_count, expert_count)
    running = (jnp.cumsum(grouped, axis=1, dtype=jnp.int32) - 1).reshape(
        row_count, top_count, expert_count
    )
    return jnp.sum(running * onehot, axis=-1, dtype=jnp.int32)


def per_device(
    tokens,
    norm_gain,
    router,
    expert_ids,
    modality,
    expert_gate,
    expert_up,
    expert_down,
    shared_gate,
    shared_up,
    shared_down,
):
    normed = rms_normed(tokens, norm_gain)
    weights = route_weights(normed, router, expert_ids)
    tok_rows, model_width = normed.shape
    top_count = expert_ids.shape[1]
    groups = lax.axis_size("expert")
    pair_count = lax.axis_size("tensor")
    dp_count = lax.axis_size("dp")
    half_width = model_width // pair_count
    expert_count = groups * expert_gate.shape[0]
    capacity = pair_count * (
        (5 * tok_rows * top_count + 4 * expert_count * pair_count - 1)
        // (4 * expert_count * pair_count)
    )
    slot_rank = capacity_slots(expert_ids, expert_count, tok_rows)
    target = expert_ids * capacity + slot_rank
    positions = jnp.arange(expert_count * capacity, dtype=jnp.int32)
    placing = jnp.any(positions[:, None, None] == target[None, :, :], axis=2).astype(jnp.bfloat16)
    outgoing = jnp.dot(placing, normed, preferred_element_type=jnp.float32).astype(jnp.bfloat16)
    outgoing = outgoing.reshape(groups, capacity, model_width)
    received = lax.all_to_all(outgoing, "expert", split_axis=0, concat_axis=0, tiled=True)
    flat_rows = received.reshape(-1, model_width)
    gate_value = jnp.dot(flat_rows, expert_gate[0], preferred_element_type=jnp.float32)
    up_value = jnp.dot(flat_rows, expert_up[0], preferred_element_type=jnp.float32)
    hidden = (jax.nn.silu(gate_value) * up_value).astype(jnp.bfloat16)
    result = jnp.dot(hidden, expert_down[0], preferred_element_type=jnp.float32)
    partials = result.reshape(received.shape[0], received.shape[1], model_width)
    reduced = sent_and_summed(partials.astype(jnp.bfloat16), "tensor", 2)
    returned = lax.all_to_all(
        reduced.astype(jnp.bfloat16), "expert", split_axis=0, concat_axis=0, tiled=True
    ).astype(reduced.dtype)
    picked = returned.reshape(-1, returned.shape[2])[target]
    routed = jnp.sum(weights[:, :, None] * picked, axis=1)
    everyone, kind_flags = (collect(normed, "dp", 0), collect(modality, "dp", 0))
    image_flag = kind_flags.astype(jnp.float32)[:, None]

    def shared_hidden(modal_index, keep):
        gate_value = jnp.dot(everyone, shared_gate[modal_index], preferred_element_type=jnp.float32)
        up_value = jnp.dot(everyone, shared_up[modal_index], preferred_element_type=jnp.float32)
        return (jax.nn.silu(gate_value) * up_value * keep).astype(jnp.bfloat16)

    joined = jnp.concatenate(
        [shared_hidden(0, image_flag), shared_hidden(1, 1.0 - image_flag)], axis=1
    )
    down_blocks = shared_down.reshape(-1, pair_count, half_width)
    split_rows = joined.reshape(dp_count, tok_rows, joined.shape[1])
    shared_term = jnp.einsum(
        "pks,std->ptkd", split_rows, down_blocks, preferred_element_type=jnp.float32
    )
    shared_sum = sent_and_summed(
        shared_term.reshape(-1, half_width).astype(jnp.bfloat16), ("dp", "tensor"), 0
    )
    total = shared_sum + routed
    return total.astype(jnp.bfloat16)


def solution(mesh):
    in_specs = (
        P(("dp", "expert"), None),
        P(),
        P(),
        P(("dp", "expert"), None),
        P(("dp", "expert")),
        P("expert", None, "tensor"),
        P("expert", None, "tensor"),
        P("expert", "tensor", None),
        P(None, None, ("dp", "tensor")),
        P(None, None, ("dp", "tensor")),
        P(None, ("dp", "tensor"), None),
    )
    out_specs = P(("dp", "expert"), "tensor")
    return jax.shard_map(
        per_device, mesh=mesh, in_specs=in_specs, out_specs=out_specs, check_vma=False
    )
```

profile of v0, /device:TPU:1, one launch (start us, length us, event | category | flops | bytes accessed | tf_op | source)
XLA Modules:
  0.0 195.9 jit_solution(18191164852900598706)
XLA Ops:
  0.0 1.4 broadcast_in_dim.11
  1.4 3.3 %all-to-all-start.1 = ((s32[2,1,128]{2,1,0:T(1,128)}), s32[2,1,128]{2,1,0:T(1,128)S(1)}, u32[]{:S(2)}, u32[]{:S(2)}) async-start(s32[2,1,128]{2,1,0:T(1,128)} %broadcast_in_dim.11), calls=%async_computation.1 | async-start | bytes 2048 | tf_op jit(solution)/shard_map/all_to_all | solution.py:23
  4.7 0.8 copy.92
  5.5 0.1 eq.40
  5.6 0.1 compare_convert_fusion
  5.6 1.2 reduce-window.6
  6.8 0.2 slice_reduce_fusion
  7.0 0.1 copy.94
  7.1 0.1 copy.95
  7.2 0.1 broadcast.88
  7.3 0.1 fusion.29
  7.4 0.1 reduce_sum.63
  7.6 0.1 copy.96
  7.6 0.7 compare_select_fusion.1
  8.3 0.2 fusion.9
  8.5 1.2 fusion.14
  9.7 1.2 fusion.16
  11.0 2.3 %convolution_convert_fusion.1 = bf16[640,2048]{1,0:T(8,128)(2,1)} fusion(pred[640,128]{1,0:T(8,128)(4,1)S(1)} %fusion.9, bf16[128,2048]{1,0:T(8,128)(2,1)S(1)} %fusion.16), kind=kOutput, calls=%fused_computation.3 | convolution fusion | flops 336855040 | bytes 3227648 | tf_op jit(solution)/shard_map/dot_general | solution.py:92
  13.3 5.2 %reshape.188 = bf16[32,20,2048]{2,1,0:T(8,128)(2,1)} reshape(bf16[640,2048]{1,0:T(8,128)(2,1)} %convolution_convert_fusion.1) | data formatting | bytes 5242880 | tf_op jit(solution)/shard_map/reshape | solution.py:93
  18.5 0.0 all-to-all-done.1
  18.5 9.5 %all-to-all-start.3 = ((bf16[32,20,2048]{2,1,0:T(8,128)(2,1)}), bf16[32,20,2048]{2,1,0:T(8,128)(2,1)}, u32[]{:S(2)}, u32[]{:S(2)}) async-start(bf16[32,20,2048]{2,1,0:T(8,128)(2,1)} %reshape.188), calls=%async_computation.3 | async-start | bytes 6291456 | tf_op jit(solution)/shard_map/all_to_all | solution.py:94
  28.0 4.7 %reshape.181 = bf16[352,2,1024]{2,1,0:T(2,128)(2,1)} reshape(bf16[2,176,2048]{2,1,0:T(8,128)(2,1)} %param.21) | data formatting | bytes 2883584 | tf_op jit(solution)/shard_map/reshape | solution.py:118
  32.7 35.1 %all-to-all-done.3 = bf16[32,20,2048]{2,1,0:T(8,128)(2,1)} async-done(((bf16[32,20,2048]{2,1,0:T(8,128)(2,1)}), bf16[32,20,2048]{2,1,0:T(8,128)(2,1)}, u32[]{:S(2)}, u32[]{:S(2)}) %all-to-all-start.3) | async-done | bytes 2621472 | tf_op jit(solution)/shard_map/all_to_all | solution.py:94
  67.8 1.2 broadcast_in_dim.10
  69.0 4.4 %all-to-all-start = ((bf16[2,128,2048]{2,1,0:T(8,128)(2,1)}), bf16[2,128,2048]{2,1,0:T(8,128)(2,1)}, u32[]{:S(2)}, u32[]{:S(2)}) async-start(bf16[2,128,2048]{2,1,0:T(8,128)(2,1)} %broadcast_in_dim.10), calls=%async_computation | async-start | bytes 2097152 | tf_op jit(solution)/shard_map/all_to_all | solution.py:23
  73.4 5.2 %reshape.189 = bf16[640,2048]{1,0:T(8,128)(2,1)} reshape(bf16[32,20,2048]{2,1,0:T(8,128)(2,1)} %all-to-all-done.3) | data formatting | bytes 5242880 | tf_op jit(solution)/shard_map/reshape | solution.py:95
  78.6 5.2 %fusion.3 = f32[640,704]{0,1:T(8,128)S(1)} fusion(bf16[640,2048]{1,0:T(8,128)(2,1)} %reshape.189, bf16[1,2048,704]{1,2,0:T(8,128)(2,1)} %param.16), kind=kOutput, calls=%fused_computation.7 | convolution fusion | flops 1845493760 | bytes 7307264 | tf_op jit(solution)/shard_map/dot_general | solution.py:96
  83.8 3.4 %multiply_convert_fusion = bf16[640,704]{0,1:T(8,128)(2,1)} fusion(f32[640,704]{0,1:T(8,128)S(1)} %fusion.3, bf16[640,2048]{1,0:T(8,128)(2,1)S(1)} %copy-done.1, bf16[1,2048,704]{1,2,0:T(8,128)(2,1)S(1)} %copy-done.3), kind=kOutput, calls=%fused_computation.12 | convolution fusion | flops 1848197120 | bytes 8208384 | tf_op jit(solution)/shard_map/dot_general | solution.py:97
  87.2 2.3 %copy.97 = bf16[640,704]{1,0:T(8,128)(2,1)} copy(bf16[640,704]{0,1:T(8,128)(2,1)} %multiply_convert_fusion) | data formatting | bytes 1802240 | tf_op jit(solution)/shard_map/convert_element_type | solution.py:98
  89.5 2.2 %dot_general.41 = bf16[32,20,704]{2,1,0:T(8,128)(2,1)} reshape(bf16[640,704]{1,0:T(8,128)(2,1)} %copy.97) | data formatting | bytes 1802240 | tf_op jit(solution)/shard_map/dot_general | solution.py:99
  91.6 3.5 %convolution_convert_fusion = bf16[32,20,2048]{2,0,1:T(8,128)(2,1)S(1)} fusion(bf16[1,704,2048]{2,1,0:T(8,128)(2,1)S(1)} %copy-done, bf16[32,20,704]{2,1,0:T(8,128)(2,1)} %dot_general.41), kind=kOutput, calls=%fused_computation.2 | convolution fusion | flops 1846804480 | bytes 6406144 | tf_op jit(solution)/shard_map/dot_general | solution.py:99
  95.1 1.8 copy.117
  96.9 0.0 all-to-all-done
  96.9 5.2 %all-to-all-start.4 = ((bf16[2,32,20,1024]{3,1,2,0:T(8,128)(2,1)}), bf16[2,32,20,1024]{3,1,2,0:T(8,128)(2,1)}, u32[]{:S(2)}, u32[]{:S(2)}) async-start(bf16[2,32,20,1024]{3,1,2,0:T(8,128)(2,1)} %bitcast.68), calls=%async_computation.4 | async-start | bytes 5242880 | tf_op jit(solution)/shard_map/all_to_all | solution.py:17
  102.1 0.0 copy-start.4
  102.1 2.0 %fusion.22 = f32[256,176]{0,1:T(8,128)S(1)} fusion(bf16[256,2048]{1,0:T(8,128)(2,1)} %bitcast, bf16[2,2048,176]{1,2,0:T(8,128)(2,1)} %param.19), kind=kOutput, calls=%fused_computation.34 | convolution fusion | flops 184549376 | bytes 1949696 | tf_op jit(solution)/shard_map/dot_general | solution.py:111
  104.2 1.9 fusion.19
  106.1 1.7 fusion.12
  107.9 1.7 fusion.13
  109.6 0.7 pad_maximum_fusion
  110.3 1.6 reshape.180
  111.9 3.2 %convolution_convert_fusion.2 = bf16[2,128,2,1024]{3,1,2,0:T(8,128)(2,1)} fusion(bf16[352,2,1024]{2,1,0:T(2,128)(2,1)} %reshape.181, bf16[2,128,352,1]{1,0,2,3:T(2,128)(2,1)} %bitcast.71), kind=kOutput, calls=%fused_computation.13 | convolution fusion | flops 369623040 | bytes 2670592 | tf_op jit(solution)/shard_map/pks,std->ptkd/dot_general | solution.py:120
  115.2 18.3 %all-to-all-done.4 = bf16[2,32,20,1024]{3,1,2,0:T(8,128)(2,1)} async-done(((bf16[2,32,20,1024]{3,1,2,0:T(8,128)(2,1)}), bf16[2,32,20,1024]{3,1,2,0:T(8,128)(2,1)}, u32[]{:S(2)}, u32[]{:S(2)}) %all-to-all-start.4) | async-done | bytes 2621472 | tf_op jit(solution)/shard_map/all_to_all | solution.py:17
  133.4 4.2 %all-to-all-start.2 = ((bf16[4,128,1024]{2,1,0:T(8,128)(2,1)}), bf16[4,128,1024]{2,1,0:T(8,128)(2,1)}, u32[]{:S(2)}, u32[]{:S(2)}) async-start(bf16[4,128,1024]{2,1,0:T(8,128)(2,1)} %bitcast.69), calls=%async_computation.2 | async-start | bytes 2097152 | tf_op jit(solution)/shard_map/all_to_all | solution.py:17
  137.7 3.8 %reduce_sum.64 = bf16[32,20,1024]{2,0,1:T(8,128)(2,1)} reduce(bf16[2,32,20,1024]{3,1,2,0:T(8,128)(2,1)} %all-to-all-done.4, bf16[]{:T(256)} %constant.46.clone.1), dimensions={0}, to_apply=%region_7.8 | reduce | flops 655360 | bytes 3932162 | tf_op jit(solution)/shard_map/reduce_sum | solution.py:18
  141.5 3.2 %copy.101 = bf16[32,20,1024]{2,1,0:T(8,128)(2,1)} copy(bf16[32,20,1024]{2,0,1:T(8,128)(2,1)} %reduce_sum.64) | data formatting | bytes 2621440 | tf_op jit(solution)/shard_map/reduce_sum | solution.py:18
  144.7 8.0 %all-to-all-done.2 = bf16[4,128,1024]{2,1,0:T(8,128)(2,1)} async-done(((bf16[4,128,1024]{2,1,0:T(8,128)(2,1)}), bf16[4,128,1024]{2,1,0:T(8,128)(2,1)}, u32[]{:S(2)}, u32[]{:S(2)}) %all-to-all-start.2) | async-done | bytes 1048608 | tf_op jit(solution)/shard_map/all_to_all | solution.py:17
  152.7 5.1 %all-to-all-start.5 = ((bf16[32,20,1024]{2,1,0:T(8,128)(2,1)}), bf16[32,20,1024]{2,1,0:T(8,128)(2,1)}, u32[]{:S(2)}, u32[]{:S(2)}) async-start(bf16[32,20,1024]{2,1,0:T(8,128)(2,1)} %copy.101), calls=%async_computation.5 | async-start | bytes 3145728 | tf_op jit(solution)/shard_map/all_to_all | solution.py:102
  157.8 0.1 copy.102
  157.9 0.1 reshape.198
  158.0 0.1 copy.89
  158.1 0.1 reshape.204
  158.2 1.2 fusion.30
  159.4 3.8 %gather_fusion.1 = f32[512]{0:T(512)S(1)} fusion(f32[128,32]{0,1:T(8,128)S(1)} %fusion.30, s32[512]{0:T(512)S(1)} %reshape.204), kind=kCustom, calls=%fused_computation.1 | custom fusion | bytes 8192 | tf_op jit(solution)/shard_map/jit(take_along_axis)/gather | solution.py:45
  163.2 0.1 reshape.207
  163.3 0.1 copy.90
  163.4 0.1 copy.91
  163.6 1.5 convert_reduce_fusion
  165.0 15.6 %all-to-all-done.5 = bf16[32,20,1024]{2,1,0:T(8,128)(2,1)} async-done(((bf16[32,20,1024]{2,1,0:T(8,128)(2,1)}), bf16[32,20,1024]{2,1,0:T(8,128)(2,1)}, u32[]{:S(2)}, u32[]{:S(2)}) %all-to-all-start.5) | async-done | bytes 1310752 | tf_op jit(solution)/shard_map/all_to_all | solution.py:102
  180.6 3.4 %reshape.195 = f32[640,1024]{1,0:T(8,128)} reshape(bf16[32,20,1024]{2,1,0:T(8,128)(2,1)} %all-to-all-done.5) | data formatting | bytes 3932160 | tf_op jit(solution)/shard_map/reshape | solution.py:105
  184.0 5.3 %gather_fusion = f32[512,1024]{1,0:T(8,128)} fusion(f32[640,1024]{1,0:T(8,128)} %reshape.195, s32[1024]{0:T(1024)S(1)} %pad_clamp_fusion), kind=kCustom, calls=%fused_computation | custom fusion | bytes 4196352 | tf_op jit(solution)/shard_map/gather | solution.py:105
  189.3 2.9 %reshape.197 = f32[128,4,1024]{2,1,0:T(4,128)} reshape(f32[512,1024]{1,0:T(8,128)} %gather_fusion) | data formatting | bytes 4194304 | tf_op jit(solution)/shard_map/gather | solution.py:105
  192.2 3.0 %multiply_reduce_fusion = f32[128,1024]{1,0:T(8,128)S(1)} fusion(f32[128,4,1024]{2,1,0:T(4,128)} %reshape.197, f32[128,4]{1,0:T(8,128)S(1)} %copy.91), kind=kLoop, calls=%fused_computation.10 | loop fusion | flops 917504 | bytes 2623488 | tf_op jit(solution)/shard_map/reduce_sum | solution.py:106
  195.2 0.8 add_convert_fusion
  (19 shorter events, 0.2 us)
Async XLA Ops:
  0.0 91.6 %copy-start = (bf16[1,704,2048]{2,1,0:T(8,128)(2,1)S(1)}, bf16[1,704,2048]{2,1,0:T(8,128)(2,1)}, u32[]{:S(2)}) copy-start(bf16[1,704,2048]{2,1,0:T(8,128)(2,1)} %param.18) | copy-start | bytes 8650756
  1.4 17.1 %all-to-all-start.1 = ((s32[2,1,128]{2,1,0:T(1,128)}), s32[2,1,128]{2,1,0:T(1,128)S(1)}, u32[]{:S(2)}, u32[]{:S(2)}) async-start(s32[2,1,128]{2,1,0:T(1,128)} %broadcast_in_dim.11), calls=%async_computation.1 | async-start | bytes 2048 | tf_op jit(solution)/shard_map/all_to_all | solution.py:23
  18.5 49.4 %all-to-all-start.3 = ((bf16[32,20,2048]{2,1,0:T(8,128)(2,1)}), bf16[32,20,2048]{2,1,0:T(8,128)(2,1)}, u32[]{:S(2)}, u32[]{:S(2)}) async-start(bf16[32,20,2048]{2,1,0:T(8,128)(2,1)} %reshape.188), calls=%async_computation.3 | async-start | bytes 6291456 | tf_op jit(solution)/shard_map/all_to_all | solution.py:94
  69.0 27.9 %all-to-all-start = ((bf16[2,128,2048]{2,1,0:T(8,128)(2,1)}), bf16[2,128,2048]{2,1,0:T(8,128)(2,1)}, u32[]{:S(2)}, u32[]{:S(2)}) async-start(bf16[2,128,2048]{2,1,0:T(8,128)(2,1)} %broadcast_in_dim.10), calls=%async_computation | async-start | bytes 2097152 | tf_op jit(solution)/shard_map/all_to_all | solution.py:23
  78.6 5.2 %copy-start.1 = (bf16[640,2048]{1,0:T(8,128)(2,1)S(1)}, bf16[640,2048]{1,0:T(8,128)(2,1)}, u32[]{:S(2)}) copy-start(bf16[640,2048]{1,0:T(8,128)(2,1)} %reshape.189) | copy-start | bytes 7864324
  78.6 5.2 %copy-start.3 = (bf16[1,2048,704]{1,2,0:T(8,128)(2,1)S(1)}, bf16[1,2048,704]{1,2,0:T(8,128)(2,1)}, u32[]{:S(2)}) copy-start(bf16[1,2048,704]{1,2,0:T(8,128)(2,1)} %param.17) | copy-start | bytes 8650756
  96.9 36.5 %all-to-all-start.4 = ((bf16[2,32,20,1024]{3,1,2,0:T(8,128)(2,1)}), bf16[2,32,20,1024]{3,1,2,0:T(8,128)(2,1)}, u32[]{:S(2)}, u32[]{:S(2)}) async-start(bf16[2,32,20,1024]{3,1,2,0:T(8,128)(2,1)} %bitcast.68), calls=%async_computation.4 | async-start | bytes 5242880 | tf_op jit(solution)/shard_map/all_to_all | solution.py:17
  102.1 4.0 %copy-start.4 = (bf16[2,2048,176]{1,2,0:T(8,128)(2,1)S(1)}, bf16[2,2048,176]{1,2,0:T(8,128)(2,1)}, u32[]{:S(2)}) copy-start(bf16[2,2048,176]{1,2,0:T(8,128)(2,1)} %param.20) | copy-start | bytes 4325380
  133.4 19.3 %all-to-all-start.2 = ((bf16[4,128,1024]{2,1,0:T(8,128)(2,1)}), bf16[4,128,1024]{2,1,0:T(8,128)(2,1)}, u32[]{:S(2)}, u32[]{:S(2)}) async-start(bf16[4,128,1024]{2,1,0:T(8,128)(2,1)} %bitcast.69), calls=%async_computation.2 | async-start | bytes 2097152 | tf_op jit(solution)/shard_map/all_to_all | solution.py:17
  144.7 13.3 %copy-start.2 = (s32[128,4]{0,1:T(4,128)S(1)}, s32[128,4]{0,1:T(4,128)}, u32[]{:S(2)}) copy-start(s32[128,4]{0,1:T(4,128)} %param.14) | copy-start | bytes 6148
  152.7 27.9 %all-to-all-start.5 = ((bf16[32,20,1024]{2,1,0:T(8,128)(2,1)}), bf16[32,20,1024]{2,1,0:T(8,128)(2,1)}, u32[]{:S(2)}, u32[]{:S(2)}) async-start(bf16[32,20,1024]{2,1,0:T(8,128)(2,1)} %copy.101), calls=%async_computation.5 | async-start | bytes 3145728 | tf_op jit(solution)/shard_map/all_to_all | solution.py:102
where the time goes:
time: 197 us; the launch traced here: 196 us
  waiting for transfers between devices  76.9 us (39%)
  local copies, waits for them, and re-layouts  46.3 us (24%)
  starting transfers between devices  31.7 us (16%)
  matrix products  26.3 us (13%)
  other arithmetic  14.5 us (7%)
    all_to_all x1, waiting for transfers between devices, per_device(): lax.all_to_all(outgoing, 'expert', split_axis=0, concat_axis=0, tiled=True)  35.1 us
    all_to_all x2, waiting for transfers between devices, sent_and_summed(): lax.all_to_all(tiles, axis, split_axis=0, concat_axis=0, tiled=True)  26.3 us
    all_to_all x1, waiting for transfers between devices, per_device(): lax.all_to_all(reduced.astype(jnp.bfloat16), 'expert', split_axis=0, conc...  15.6 us
    all_to_all x1, starting transfers between devices, per_device(): lax.all_to_all(outgoing, 'expert', split_axis=0, concat_axis=0, tiled=True)  9.55 us
    all_to_all x2, starting transfers between devices, sent_and_summed(): lax.all_to_all(tiles, axis, split_axis=0, concat_axis=0, tiled=True)  9.41 us
    gather x2, local copies, waits for them, and re-layouts, per_device(): picked = returned.reshape(-1, returned.shape[2])[target]  8.21 us
    all_to_all x2, starting transfers between devices, sent_to_all(): lax.all_to_all(jnp.broadcast_to(x[None], (size, *x.shape)), axis, 0, 0, t...  7.7 us
    reduce_sum x2, other arithmetic, sent_and_summed(): return arrived.astype(jnp.float32).sum(axis=0)  5.28 us
  transfers between devices with their start and end apart: 6, of which 4 were waited for; matrix products, arithmetic and copies ran while one was open for 35% of the time, Pallas kernels for 0%

commit v1 on v0

v1 whole, which is shorter than its diff:
```python
import jax
import jax.numpy as jnp
from jax import lax
from jax.experimental import pallas as pl
from jax.experimental.pallas import tpu as pltpu
from jax.sharding import PartitionSpec as P

MESH = pl.DeviceIdType.MESH
F32, BF16 = jnp.float32, jnp.bfloat16
RING = 4
EPS = 1e-06
UNPICKED = -100.0
ORDER = (0, 1, 3, 2)


def dot(a, b):
    return lax.dot_general(a, b, (((1,), (0,)), ((), ())), preferred_element_type=F32)


def silu(v):
    return v / (1.0 + jnp.exp(-v))


def kernel(
    tokens, gain, router, ids, flags, gate_h, up_h, down_h, sgate_h, sup_h, sdown_h, out,
    gate, up, down, sgate, sup, sdown,
    ag, meta, sel, place, weigh, slots, recv, gacc, uacc, hid, yout, back, rs_out, rs_in,
    x_out, x_in, sown, soth, sh_in, xfer_out, xfer_in, own,
    w_sem, g_s, g_r, m_s, m_r, xs_s, xs_r, d_s, d_r, b_s, b_r, r_s, r_r, sh_s, sh_r, t_s, t_r,
):
    rows, width = tokens.shape
    half = width // 2
    cap = recv.shape[0] // 32
    slab = RING * cap
    dp, me, tp = lax.axis_index("dp"), lax.axis_index("expert"), lax.axis_index("tensor")
    y, z, c = me // 8, (me % 8) // 2, me % 2
    dpo, tpo = 1 - dp, 1 - tp

    def at(yy, zz, cc):
        return (dp, yy * 8 + zz * 2 + cc, tp)

    def along_y(k):
        return (y + k) % RING

    def along_z(k):
        return (z + k) % RING

    def ring1(k):
        return at(c * along_y(k) + (1 - c) * y, (1 - c) * along_z(k) + c * z, c)

    def expert_of(k, cc):
        return (c * y + (1 - c) * along_y(k)) * 8 + (c * along_z(k) + (1 - c) * z) * 2 + cc

    def ring2(k, cc):
        return (dp, expert_of(k, cc), tp)

    def source(k, cs):
        return at(along_y(RING - k), z, 0) if cs == 0 else at(y, along_z(RING - k), 1)

    def mult(v, m):
        return pl.multiple_of(v, m)

    loads = [
        pltpu.make_async_copy(s, d, w_sem.at[i])
        for i, (s, d) in enumerate(
            [(sgate_h, sgate), (sup_h, sup), (sdown_h, sdown), (gate_h.at[0], gate), (up_h.at[0], up), (down_h.at[0], down)]
        )
    ]
    for cp in loads:
        cp.start()

    barrier = pltpu.get_barrier_semaphore()
    peers = [at(y, z, 1 - c), (dpo, me, 0), (dpo, me, 1), (dp, me, tpo)]
    for k in range(1, RING):
        for cc in range(2):
            peers += [at(along_y(k), z, cc), at(y, along_z(k), cc)]
    for peer in peers:
        pl.semaphore_signal(barrier, inc=1, device_id=peer, device_id_type=MESH)

    def remote(src, dst, ssem, rsem, dev):
        return pltpu.make_async_remote_copy(
            src_ref=src, dst_ref=dst, send_sem=ssem, recv_sem=rsem, device_id=dev, device_id_type=MESH
        )

    step = 32

    def norm_rows(i, carry):
        at_rows = pl.ds(mult(i * step, step), step)
        v = tokens[at_rows, :].astype(F32)
        inv = lax.rsqrt(jnp.mean(v * v, axis=-1, keepdims=True) + EPS)
        ag[at_rows, :] = (v * inv * gain[...]).astype(BF16)
        return carry

    lax.fori_loop(0, rows // step, norm_rows, 0)
    pl.semaphore_wait(barrier, len(peers))

    def cols(h):
        return pl.ds(h * half, half)

    def gather(h, j):
        return remote(
            ag.at[pl.ds(0, rows), cols(h)], ag.at[pl.ds(j * rows, rows), cols(h)], g_s.at[h, j], g_r.at[h, j], ring1(j)
        )

    for j in (2, 1, 3):
        gather(0, j).start()

    mine = pl.ds(mult(tp * half, half), half)
    theirs = pl.ds(mult(tpo * half, half), half)
    flag_rows = jnp.transpose(jnp.broadcast_to(flags[...].astype(F32), (rows, rows)))
    x_out[:, pl.ds(0, half)] = ag[pl.ds(0, rows), mine]
    x_out[:, pl.ds(half, 128)] = flag_rows.astype(BF16)

    def dp_rows(t):
        return remote(x_out, x_in.at[tp], xs_s.at[t], xs_r.at[tp], (dpo, me, t))

    def dp_rows_in(t):
        return remote(x_out, x_in.at[t], xs_s.at[t], xs_r.at[t], (dpo, me, t))

    for t in range(2):
        dp_rows(t).start()

    lane = lax.broadcasted_iota(jnp.int32, (rows, 128), 1)
    sub = lax.broadcasted_iota(jnp.int32, (rows, 128), 0)
    chosen = jnp.zeros((rows, 128), F32)
    for k in range(ids.shape[1]):
        chosen = chosen + (ids[:, k : k + 1] == lane).astype(F32)
    earlier = (lane < sub).astype(BF16)
    rank = dot(earlier, chosen.astype(BF16))
    logits = dot(ag[pl.ds(0, rows), :], router[...])
    score = chosen[:, :32] / (1.0 + jnp.exp(-logits))
    weight = score / jnp.sum(score, axis=1, keepdims=True)
    shift = (
        lax.broadcasted_iota(jnp.int32, (32, 128), 1) == lax.broadcasted_iota(jnp.int32, (32, 128), 0) + 32
    ).astype(BF16)
    moved = dot(weight.astype(BF16), shift)
    ranked = jnp.where(chosen > 0.0, rank, UNPICKED)
    meta[pl.ds(0, rows), :] = jnp.where(lane < 32, ranked, moved).astype(BF16)

    def meta_copy(j):
        return remote(meta.at[pl.ds(0, rows)], meta.at[pl.ds(j * rows, rows)], m_s.at[j], m_r.at[j], ring1(j))

    for j in (2, 1, 3):
        meta_copy(j).start()
    for j in (2, 1, 3):
        gather(1, j).start()

    for cp in loads[:3]:
        cp.wait()

    def shared(read_rows, keep, write):
        hidden = []
        for m in range(2):
            g = jnp.zeros((rows, sgate.shape[2]), F32)
            u = jnp.zeros((rows, sgate.shape[2]), F32)
            for h in range(2):
                part = read_rows(h)
                g = g + dot(part, sgate[m, cols(h), :])
                u = u + dot(part, sup[m, cols(h), :])
            picked = keep if m == 0 else 1.0 - keep
            hidden.append((silu(g) * u * picked).astype(BF16))
        for h in range(2):
            write(h, dot(hidden[0], sdown[0, :, cols(h)]) + dot(hidden[1], sdown[1, :, cols(h)]))

    def write_own(h, v):
        sown[:, cols(h)] = v

    shared(lambda h: ag[pl.ds(0, rows), cols(h)], flag_rows[:, :1], write_own)

    for s in range(8):
        e = expert_of(s // 2, s % 2)
        sel[pl.ds(s * slab, slab), :] = (lax.broadcasted_iota(jnp.int32, (slab, 128), 1) == e).astype(BF16)
    for j in (2, 1, 3):
        meta_copy(j).wait_recv()
    slot_row = lax.broadcasted_iota(jnp.int32, (slab, rows), 0).astype(F32)
    col = lax.broadcasted_iota(jnp.int32, (1, 8 * slab), 1)
    e_col = jnp.zeros((1, 8 * slab), jnp.int32)
    r_col = col
    for s in range(8):
        inside = (col >= s * slab) & (col < (s + 1) * slab)
        e_col = jnp.where(inside, expert_of(s // 2, s % 2), e_col)
        r_col = jnp.where(inside, col - s * slab, r_col)
    r_col = r_col.astype(F32)
    wide = lax.broadcasted_iota(jnp.int32, (128, 8 * slab), 0)
    sel_pos = (wide == e_col).astype(BF16)
    sel_w = (wide == e_col + 32).astype(BF16)
    for j in range(RING):
        block = meta[pl.ds(j * rows, rows), :]
        turned = jnp.transpose(block.astype(F32)).astype(BF16)
        turned_pos = dot(sel[...], turned)
        for s in range(8):
            part = turned_pos[s * slab : (s + 1) * slab, :]
            place[pl.ds(s * slab, slab), pl.ds(j * rows, rows)] = jnp.where(
                part == slot_row - float(cap * j), 1.0, 0.0
            ).astype(BF16)
        pos = dot(block, sel_pos)
        wts = dot(block, sel_w)
        weigh[pl.ds(j * rows, rows), :] = jnp.where(pos == r_col - float(cap * j), wts, 0.0).astype(BF16)

    def slot_rows(k, cc):
        return pl.ds(k * 2 * slab + mult(cc * slab, slab), slab)

    def dispatch(h, k, cc):
        return remote(
            slots.at[slot_rows(k, cc), cols(h)],
            recv.at[slot_rows(k, c), cols(h)],
            d_s.at[h, k * 2 + cc],
            d_r.at[h, k * 2 + c],
            ring2(k, cc),
        )

    def dispatch_in(h, k, cs):
        return remote(
            slots.at[slot_rows(k, cs), cols(h)],
            recv.at[slot_rows(k, cs), cols(h)],
            d_s.at[h, k * 2 + cs],
            d_r.at[h, k * 2 + cs],
            source(k, cs) if k else at(y, z, 1 - c),
        )

    def send_slots(h):
        for k in (2, 1, 3, 0):
            both = pl.ds(k * 2 * slab, 2 * slab)
            slots[both, cols(h)] = dot(place[both, :], ag[:, cols(h)]).astype(BF16)
            if k:
                for cc in range(2):
                    dispatch(h, k, cc).start()
            else:
                dispatch(h, 0, 1 - c).start()
                recv[slot_rows(0, c), cols(h)] = slots[slot_rows(0, c), cols(h)]

    def await_slots(h, k):
        if k:
            for cs in range(2):
                dispatch_in(h, k, cs).wait_recv()
        else:
            dispatch_in(h, 0, 1 - c).wait_recv()

    for j in (2, 1, 3):
        gather(0, j).wait_recv()
    send_slots(0)

    for t in range(2):
        dp_rows_in(t).wait_recv()

    def write_other(h, v):
        soth[h] = v.astype(BF16)

    shared(lambda h: x_in[h, :, pl.ds(0, half)], x_in[0, :, pl.ds(half, 128)][:, :1].astype(F32), write_other)

    def shared_back(t):
        return remote(soth.at[t], sh_in.at[tp], sh_s.at[t], sh_r.at[tp], (dpo, me, t))

    def shared_in(t):
        return remote(soth.at[t], sh_in.at[t], sh_s.at[t], sh_r.at[t], (dpo, me, t))

    for t in range(2):
        shared_back(t).start()

    for cp in loads[3:]:
        cp.wait()

    def first_half(k):
        await_slots(0, k)
        both = pl.ds(k * 2 * slab, 2 * slab)
        gacc[both, :] = dot(recv[both, cols(0)], gate[cols(0), :])
        uacc[both, :] = dot(recv[both, cols(0)], up[cols(0), :])

    first_half(0)
    for j in (2, 1, 3):
        gather(1, j).wait_recv()
    send_slots(1)
    for k in (1, 3, 2):
        first_half(k)

    def ret(f, fcols, k, cs):
        return remote(
            yout.at[slot_rows(k, cs), fcols],
            back.at[slot_rows(k, c), fcols],
            b_s.at[f, k * 2 + cs],
            b_r.at[f, k * 2 + c],
            source(k, cs) if k else at(y, z, 1 - c),
        )

    def ret_in(f, fcols, k, cc):
        return remote(
            yout.at[slot_rows(k, cc), fcols],
            back.at[slot_rows(k, cc), fcols],
            b_s.at[f, k * 2 + cc],
            b_r.at[f, k * 2 + cc],
            ring2(k, cc),
        )

    def project(f, fcols, k):
        both = pl.ds(k * 2 * slab, 2 * slab)
        yout[both, fcols] = dot(hid[both, :], down[:, fcols]).astype(BF16)
        if k:
            for cs in range(2):
                ret(f, fcols, k, cs).start()
        else:
            ret(f, fcols, 0, 1 - c).start()
            back[slot_rows(0, c), fcols] = yout[slot_rows(0, c), fcols]

    for k in ORDER:
        await_slots(1, k)
        both = pl.ds(k * 2 * slab, 2 * slab)
        g = gacc[both, :] + dot(recv[both, cols(1)], gate[cols(1), :])
        u = uacc[both, :] + dot(recv[both, cols(1)], up[cols(1), :])
        hid[both, :] = (silu(g) * u).astype(BF16)
        project(0, theirs, k)
    for k in ORDER:
        project(1, mine, k)

    def reduce(f, j):
        return remote(rs_out.at[f, j], rs_in.at[f, j], r_s.at[f, j], r_r.at[f, j], ring1((RING - j) % RING))

    def transfer():
        return remote(xfer_out, xfer_in, t_s, t_r, (dp, me, tpo))

    for f, fcols in ((0, theirs), (1, mine)):
        for k in ORDER:
            for cc in range(2) if k else (1 - c,):
                ret_in(f, fcols, k, cc).wait_recv()
        for j in (2, 1, 3):
            rs_out[f, j] = dot(weigh[pl.ds(j * rows, rows), :], back[:, fcols]).astype(BF16)
            reduce(f, j).start()
        own[f] = dot(weigh[pl.ds(0, rows), :], back[:, fcols]) + sown[:, fcols]

    def total(f):
        for j in (1, 3, 2):
            reduce(f, j).wait_recv()
        return own[f] + rs_in[f, 1].astype(F32) + rs_in[f, 3].astype(F32) + rs_in[f, 2].astype(F32)

    xfer_out[...] = total(0).astype(BF16)
    transfer().start()
    for t in range(2):
        shared_in(t).wait_recv()
    own[1] = total(1) + sh_in[0].astype(F32) + sh_in[1].astype(F32)
    transfer().wait_recv()
    out[...] = (own[1] + xfer_in[...].astype(F32)).astype(BF16)

    for h in range(2):
        for j in (2, 1, 3):
            gather(h, j).wait_send()
            reduce(h, j).wait_send()
        for k in range(1, RING):
            for cc in range(2):
                dispatch(h, k, cc).wait_send()
                ret(h, theirs, k, cc).wait_send()
        dispatch(h, 0, 1 - c).wait_send()
        ret(h, theirs, 0, 1 - c).wait_send()
        dp_rows(h).wait_send()
        shared_back(h).wait_send()
    for j in (2, 1, 3):
        meta_copy(j).wait_send()
    transfer().wait_send()


def per_device(
    tokens, norm_gain, router, expert_ids, modality, expert_gate, expert_up, expert_down, shared_gate, shared_up, shared_down
):
    rows, width = tokens.shape
    half = width // 2
    cap = 20
    hidden = expert_gate.shape[2]
    slot_count = 32 * cap
    dma = pltpu.SemaphoreType.DMA
    vm = pltpu.VMEM
    return pl.pallas_call(
        kernel,
        out_shape=jax.ShapeDtypeStruct((rows, half), BF16),
        in_specs=[pl.BlockSpec(memory_space=pltpu.VMEM)] * 5 + [pl.BlockSpec(memory_space=pl.ANY)] * 6,
        out_specs=pl.BlockSpec(memory_space=pltpu.VMEM),
        scratch_shapes=[
            vm(expert_gate.shape[1:], BF16),
            vm(expert_up.shape[1:], BF16),
            vm(expert_down.shape[1:], BF16),
            vm(shared_gate.shape, BF16),
            vm(shared_up.shape, BF16),
            vm(shared_down.shape, BF16),
            vm((RING * rows, width), BF16),
            vm((RING * rows, 128), BF16),
            vm((slot_count, 128), BF16),
            vm((slot_count, RING * rows), BF16),
            vm((RING * rows, slot_count), BF16),
            vm((slot_count, width), BF16),
            vm((slot_count, width), BF16),
            vm((slot_count, hidden), F32),
            vm((slot_count, hidden), F32),
            vm((slot_count, hidden), BF16),
            vm((slot_count, width), BF16),
            vm((slot_count, width), BF16),
            vm((2, RING, rows, half), BF16),
            vm((2, RING, rows, half), BF16),
            vm((rows, half + 128), BF16),
            vm((2, rows, half + 128), BF16),
            vm((rows, width), F32),
            vm((2, rows, half), BF16),
            vm((2, rows, half), BF16),
            vm((rows, half), BF16),
            vm((rows, half), BF16),
            vm((2, rows, half), F32),
            dma((6,)),
            dma((2, RING)), dma((2, RING)),
            dma((RING,)), dma((RING,)),
            dma((2,)), dma((2,)),
            dma((2, 8)), dma((2, 8)),
            dma((2, 8)), dma((2, 8)),
            dma((2, RING)), dma((2, RING)),
            dma((2,)), dma((2,)),
            dma, dma,
        ],
        compiler_params=pltpu.CompilerParams(
            collective_id=0, has_side_effects=True, vmem_limit_bytes=60 * 1024 * 1024
        ),
        name="moe_layer",
    )(
        tokens, norm_gain.reshape(1, width), router, expert_ids, modality.reshape(1, rows),
        expert_gate, expert_up, expert_down, shared_gate, shared_up, shared_down,
    )


def solution(mesh):
    in_specs = (
        P(("dp", "expert"), None),
        P(),
        P(),
        P(("dp", "expert"), None),
        P(("dp", "expert")),
        P("expert", None, "tensor"),
        P("expert", None, "tensor"),
        P("expert", "tensor", None),
        P(None, None, ("dp", "tensor")),
        P(None, None, ("dp", "tensor")),
        P(None, ("dp", "tensor"), None),
    )
    out_specs = P(("dp", "expert"), "tensor")
    return jax.shard_map(per_device, mesh=mesh, in_specs=in_specs, out_specs=out_specs, check_vma=False)
```

time: 197 us -> 94.3 us (0.48)
  waiting for transfers between devices: 76.9 us -> 0 us
  Pallas kernels: 0 us -> 73.9 us
  starting transfers between devices: 31.7 us -> 0 us
  local copies, waits for them, and re-layouts: 46.3 us -> 19.9 us
  matrix products: 26.3 us -> 0 us
  other arithmetic: 14.5 us -> 0 us
    all_to_all x6 -> x0, waiting for transfers between devices: 76.9 us -> none  [the longest x1 35.1 us: per_device(): lax.all_to_all(outgoing, 'expert', split_axis=0, concat_axis=0, tiled=True)]
    pallas_call x0 -> x1, Pallas kernels: none -> 73.9 us  [per_device(): pl.pallas_call(kernel, out_shape=jax.ShapeDtypeStruct((rows, half), BF16)...]
    all_to_all x6 -> x0, starting transfers between devices: 31.7 us -> none  [the longest x1 9.55 us: per_device(): lax.all_to_all(outgoing, 'expert', split_axis=0, concat_axis=0, tiled=True)]
    dot_general x10 -> x0, matrix products: 26.3 us -> none  [the longest x1 5.18 us: per_device(): jnp.dot(flat_rows, expert_gate[0], preferred_element_type=jnp.float32)]
    reshape x6 -> x0, local copies, waits for them, and re-layouts: 21.9 us -> none  [the longest x1 5.19 us: per_device(): flat_rows = received.reshape(-1, model_width)]
    unnamed x11 -> x9, local copies, waits for them, and re-layouts: 0.81 us -> 19.9 us
    gather x7 -> x0, local copies, waits for them, and re-layouts: 12.3 us -> none  [the longest x2 8.21 us: per_device(): picked = returned.reshape(-1, returned.shape[2])[target]]
    reduce_sum x6 -> x0, other arithmetic: 9.65 us -> none  [the longest x2 5.28 us: sent_and_summed(): return arrived.astype(jnp.float32).sum(axis=0)]
  transfers between devices with their start and end apart: 6 -> 0, of which waited for: 4 -> 0; matrix products, arithmetic and copies ran while one was open for 35% -> 0% of each run, Pallas kernels for 0% -> 0%
where the time goes in v1:
time: 94.3 us; the launch traced here: 93.9 us
  Pallas kernels  73.9 us (78%)
  local copies, waits for them, and re-layouts  19.9 us (21%)
    pallas_call x1, Pallas kernels, per_device(): pl.pallas_call(kernel, out_shape=jax.ShapeDtypeStruct((rows, half), BF16)...  73.9 us
    unnamed x9, local copies, waits for them, and re-layouts  19.9 us

profile of v1, /device:TPU:1, one launch (start us, length us, event | category | flops | bytes accessed | tf_op | source)
XLA Modules:
  0.0 93.9 jit_solution(15839152776402456334)
XLA Ops:
  0.0 1.4 %copy.13.ids = s32[128,4]{1,0:T(8,128)} copy(s32[128,4]{0,1:T(4,128)} %param.14) | data formatting | bytes 4096 | tf_op args[3]
  1.4 1.9 %copy.12.router = bf16[2048,32]{1,0:T(8,128)(2,1)} copy(bf16[2048,32]{0,1:T(8,128)(2,1)} %param.13) | data formatting | bytes 262144 | tf_op args[2]
  3.4 0.0 copy-start
  3.4 3.8 %copy.16.sgate_h = bf16[2,2048,176]{2,1,0:T(8,128)(2,1)} copy(bf16[2,2048,176]{1,2,0:T(8,128)(2,1)} %param.19) | data formatting | bytes 2883584 | tf_op args[8]
  7.2 3.7 %copy.17.sup_h = bf16[2,2048,176]{2,1,0:T(8,128)(2,1)} copy(bf16[2,2048,176]{1,2,0:T(8,128)(2,1)} %param.20) | data formatting | bytes 2883584 | tf_op args[9]
  10.8 0.0 copy-done
  10.8 2.8 %copy.14.gate_h = bf16[1,2048,704]{2,1,0:T(8,128)(2,1)} copy(bf16[1,2048,704]{1,2,0:T(8,128)(2,1)S(1)} %copy-done) | data formatting | bytes 5767168 | tf_op args[5]
  13.6 4.6 %copy.15.up_h = bf16[1,2048,704]{2,1,0:T(8,128)(2,1)} copy(bf16[1,2048,704]{1,2,0:T(8,128)(2,1)} %param.17) | data formatting | bytes 5767168 | tf_op args[6]
  18.3 73.9 %moe_layer.1 = bf16[128,1024]{1,0:T(8,128)(2,1)} custom-call(bf16[128,2048]{1,0:T(8,128)(2,1)} %tokens.1, f32[1,2048]{1,0:T(1,128)} %bitcast.2, bf16[2048,32]{1,0:T(8,128)(2,1)} %copy.12.router, s32[128,4]{1,0:T(8,128)} %copy.13.ids, s32[1,128]{1,0:T(1,128)} %bitcast.3, bf16[1,2048,704]{2,1,0:T(8,128)(2,1)} %copy.14.gate_h, ...), custom_call_target="tpu_custom_call" | custom-call | tf_op jit(solution)/shard_map/moe_layer/pallas_call | solution.py:369
  92.2 1.7 %copy.19 = bf16[128,1024]{1,0:T(8,128)(2,1)} copy(bf16[128,1024]{1,0:T(8,128)(2,1)} %moe_layer.1) | data formatting | bytes 524288
Async XLA Ops:
  3.4 7.5 %copy-start = (bf16[1,2048,704]{1,2,0:T(8,128)(2,1)S(1)}, bf16[1,2048,704]{1,2,0:T(8,128)(2,1)}, u32[]{:S(2)}) copy-start(bf16[1,2048,704]{1,2,0:T(8,128)(2,1)} %param.16) | copy-start | bytes 8650756

commit v2 on v1

--- a/solution.py
+++ b/solution.py
@@ -15,6 +15,10 @@
 
 def dot(a, b):
     return lax.dot_general(a, b, (((1,), (0,)), ((), ())), preferred_element_type=F32)
+
+
+def dot_t(a, b):
+    return lax.dot_general(a, b, (((1,), (1,)), ((), ())), preferred_element_type=F32)
 
 
 def silu(v):
@@ -120,25 +124,21 @@
     for t in range(2):
         dp_rows(t).start()
 
-    lane = lax.broadcasted_iota(jnp.int32, (rows, 128), 1)
-    sub = lax.broadcasted_iota(jnp.int32, (rows, 128), 0)
-    chosen = jnp.zeros((rows, 128), F32)
-    for k in range(ids.shape[1]):
-        chosen = chosen + (ids[:, k : k + 1] == lane).astype(F32)
-    earlier = (lane < sub).astype(BF16)
-    rank = dot(earlier, chosen.astype(BF16))
-    logits = dot(ag[pl.ds(0, rows), :], router[...])
-    score = chosen[:, :32] / (1.0 + jnp.exp(-logits))
-    weight = score / jnp.sum(score, axis=1, keepdims=True)
-    shift = (
-        lax.broadcasted_iota(jnp.int32, (32, 128), 1) == lax.broadcasted_iota(jnp.int32, (32, 128), 0) + 32
-    ).astype(BF16)
-    moved = dot(weight.astype(BF16), shift)
-    ranked = jnp.where(chosen > 0.0, rank, UNPICKED)
-    meta[pl.ds(0, rows), :] = jnp.where(lane < 32, ranked, moved).astype(BF16)
+    lane = lax.broadcasted_iota(jnp.int32, (rows, rows), 1)
+    sub = lax.broadcasted_iota(jnp.int32, (rows, rows), 0)
+    expert_row = lax.broadcasted_iota(jnp.int32, (32, rows), 0)
+    chosen = jnp.zeros((32, rows), F32)
+    for k in range(ids.shape[0]):
+        chosen = chosen + (ids[k : k + 1, :] == expert_row).astype(F32)
+    earlier = (sub < lane).astype(BF16)
+    rank = dot(chosen.astype(BF16), earlier)
+    logits = dot_t(router[...], ag[pl.ds(0, rows), :])
+    score = chosen / (1.0 + jnp.exp(-logits))
+    meta[pl.ds(0, 32), :] = jnp.where(chosen > 0.0, rank, UNPICKED).astype(BF16)
+    meta[pl.ds(32, 32), :] = (score / jnp.sum(score, axis=0, keepdims=True)).astype(BF16)
 
     def meta_copy(j):
-        return remote(meta.at[pl.ds(0, rows)], meta.at[pl.ds(j * rows, rows)], m_s.at[j], m_r.at[j], ring1(j))
+        return remote(meta.at[pl.ds(0, 64)], meta.at[pl.ds(j * 64, 64)], m_s.at[j], m_r.at[j], ring1(j))
 
     for j in (2, 1, 3):
         meta_copy(j).start()
@@ -151,12 +151,12 @@
     def shared(read_rows, keep, write):
         hidden = []
         for m in range(2):
-            g = jnp.zeros((rows, sgate.shape[2]), F32)
-            u = jnp.zeros((rows, sgate.shape[2]), F32)
+            g = jnp.zeros((rows, sgate.shape[1]), F32)
+            u = jnp.zeros((rows, sgate.shape[1]), F32)
             for h in range(2):
                 part = read_rows(h)
-                g = g + dot(part, sgate[m, cols(h), :])
-                u = u + dot(part, sup[m, cols(h), :])
+                g = g + dot_t(part, sgate[m, :, cols(h)])
+                u = u + dot_t(part, sup[m, :, cols(h)])
             picked = keep if m == 0 else 1.0 - keep
             hidden.append((silu(g) * u * picked).astype(BF16))
         for h in range(2):
@@ -169,7 +169,7 @@
 
     for s in range(8):
         e = expert_of(s // 2, s % 2)
-        sel[pl.ds(s * slab, slab), :] = (lax.broadcasted_iota(jnp.int32, (slab, 128), 1) == e).astype(BF16)
+        sel[pl.ds(s * slab, slab), :] = (lax.broadcasted_iota(jnp.int32, (slab, 64), 1) == e).astype(BF16)
     for j in (2, 1, 3):
         meta_copy(j).wait_recv()
     slot_row = lax.broadcasted_iota(jnp.int32, (slab, rows), 0).astype(F32)
@@ -185,8 +185,8 @@
     sel_pos = (wide == e_col).astype(BF16)
     sel_w = (wide == e_col + 32).astype(BF16)
     for j in range(RING):
-        block = meta[pl.ds(j * rows, rows), :]
-        turned = jnp.transpose(block.astype(F32)).astype(BF16)
+        turned = meta[pl.ds(j * 64, 64), :]
+        block = jnp.transpose(jnp.concatenate([turned.astype(F32)] * 2, axis=0)).astype(BF16)
         turned_pos = dot(sel[...], turned)
         for s in range(8):
             part = turned_pos[s * slab : (s + 1) * slab, :]
@@ -263,8 +263,8 @@
     def first_half(k):
         await_slots(0, k)
         both = pl.ds(k * 2 * slab, 2 * slab)
-        gacc[both, :] = dot(recv[both, cols(0)], gate[cols(0), :])
-        uacc[both, :] = dot(recv[both, cols(0)], up[cols(0), :])
+        gacc[both, :] = dot_t(recv[both, cols(0)], gate[:, cols(0)])
+        uacc[both, :] = dot_t(recv[both, cols(0)], up[:, cols(0)])
 
     first_half(0)
     for j in (2, 1, 3):
@@ -304,8 +304,8 @@
     for k in ORDER:
         await_slots(1, k)
         both = pl.ds(k * 2 * slab, 2 * slab)
-        g = gacc[both, :] + dot(recv[both, cols(1)], gate[cols(1), :])
-        u = uacc[both, :] + dot(recv[both, cols(1)], up[cols(1), :])
+        g = gacc[both, :] + dot_t(recv[both, cols(1)], gate[:, cols(1)])
+        u = uacc[both, :] + dot_t(recv[both, cols(1)], up[:, cols(1)])
         hid[both, :] = (silu(g) * u).astype(BF16)
         project(0, theirs, k)
     for k in ORDER:
@@ -363,6 +363,7 @@
     half = width // 2
     cap = 20
     hidden = expert_gate.shape[2]
+    part = shared_gate.shape[2]
     slot_count = 32 * cap
     dma = pltpu.SemaphoreType.DMA
     vm = pltpu.VMEM
@@ -372,15 +373,15 @@
         in_specs=[pl.BlockSpec(memory_space=pltpu.VMEM)] * 5 + [pl.BlockSpec(memory_space=pl.ANY)] * 6,
         out_specs=pl.BlockSpec(memory_space=pltpu.VMEM),
         scratch_shapes=[
-            vm(expert_gate.shape[1:], BF16),
-            vm(expert_up.shape[1:], BF16),
-            vm(expert_down.shape[1:], BF16),
-            vm(shared_gate.shape, BF16),
-            vm(shared_up.shape, BF16),
+            vm((hidden, width), BF16),
+            vm((hidden, width), BF16),
+            vm((hidden, width), BF16),
+            vm((2, part, width), BF16),
+            vm((2, part, width), BF16),
             vm(shared_down.shape, BF16),
             vm((RING * rows, width), BF16),
-            vm((RING * rows, 128), BF16),
-            vm((slot_count, 128), BF16),
+            vm((RING * 64, rows), BF16),
+            vm((slot_count, 64), BF16),
             vm((slot_count, RING * rows), BF16),
             vm((RING * rows, slot_count), BF16),
             vm((slot_count, width), BF16),
@@ -415,8 +416,9 @@
         ),
         name="moe_layer",
     )(
-        tokens, norm_gain.reshape(1, width), router, expert_ids, modality.reshape(1, rows),
-        expert_gate, expert_up, expert_down, shared_gate, shared_up, shared_down,
+        tokens, norm_gain.reshape(1, width), router.T, expert_ids.T, modality.reshape(1, rows),
+        expert_gate.swapaxes(1, 2), expert_up.swapaxes(1, 2), expert_down,
+        shared_gate.swapaxes(1, 2), shared_up.swapaxes(1, 2), shared_down,
     )
 
 

time: 94.3 us -> 76.1 us (0.81)
  local copies, waits for them, and re-layouts: 19.9 us -> 1.67 us
    unnamed x9 -> x1, local copies, waits for them, and re-layouts: 19.9 us -> 1.67 us
where the time goes in v2:
time: 76.1 us; the launch traced here: 75.9 us
  Pallas kernels  74.2 us (98%)
  local copies, waits for them, and re-layouts  1.67 us (2%)
    pallas_call x1, Pallas kernels, per_device(): pl.pallas_call(kernel, out_shape=jax.ShapeDtypeStruct((rows, half), BF16)...  74.2 us
    unnamed x1, local copies, waits for them, and re-layouts  1.67 us

profile of v2, /device:TPU:1, one launch (start us, length us, event | category | flops | bytes accessed | tf_op | source)
XLA Modules:
  0.0 75.9 jit_solution(11256488779625012859)
XLA Ops:
  0.0 74.2 %moe_layer.1 = bf16[128,1024]{1,0:T(8,128)(2,1)} custom-call(bf16[128,2048]{1,0:T(8,128)(2,1)} %tokens.1, f32[1,2048]{1,0:T(1,128)} %bitcast.13, bf16[32,2048]{1,0:T(8,128)(2,1)} %bitcast.12, s32[4,128]{1,0:T(4,128)} %bitcast.14, s32[1,128]{1,0:T(1,128)} %bitcast.15, bf16[1,704,2048]{2,1,0:T(8,128)(2,1)} %bitcast.8, bf16[1,704,2048]{2,1,0:T(8,128)(2,1)} %bitcast.9, ...), custom_call_target="tpu_custom_call" | custom-call | tf_op jit(solution)/shard_map/moe_layer/pallas_call | solution.py:370
  74.2 1.7 %copy.13 = bf16[128,1024]{1,0:T(8,128)(2,1)} copy(bf16[128,1024]{1,0:T(8,128)(2,1)} %moe_layer.1) | data formatting | bytes 524288
